TPU v7x, 32 devices: a whole 2x2x4 slice. The times are simulated.
32 devices in a mesh: gx: 8 (over z, core), gy: 2 (over y), gz: 2 (over x).
Axes of the slice: x: 2, y: 2, z: 4, core: 2. Of those that a mesh axis runs over, the one named last changes fastest.
Arguments:
- load_current: float32 [384, 4096], P('gy', 'gx'), may hold values from 0 to 90
- sink_mask: int32 [384, 4096], P('gy', 'gx'), may hold values 0 or 1
- pad_mask: int32 [384, 4096], P('gy', 'gx'), may hold values from 0 to 1, as said below
- plane_class: int32 [4, 384, 4096], P('gz', 'gy', 'gx'), may hold values from 0 to 7
- via_class: int32 [4, 384, 4096], P('gz', 'gy', 'gx'), may hold values from 0 to 7
- plane_table: float32 [4, 8], P('gz'), may hold values from 0.25 to 4
- via_table: float32 [4, 8], P('gz'), may hold values from 0.25 to 4
Outputs:
- voltage: float32 [4, 384, 4096], P('gz', 'gy', 'gx')
- residual: float32 [4, 384, 4096], P('gz', 'gy', 'gx')
Inputs may be any that keep to these rules, and one draw needn't show every extreme that they name: `pad_mask`: exactly one pad in each aligned 8 x 8 tile of nodes.
All inputs are finite; a program needn't handle non-finite values. No bound on the sum of `sink_mask` on one device may be relied on, other than what follows from the above.
Results may differ from a plain program's by a relative error of at most 0.00012.
Values sent between devices are 32-bit elements; how exact they have to be, the bound alone decides.
A program may use at most 64 MiB of HBM per device.

v0:
```python
import functools

import jax
import jax.numpy as jnp
from jax import lax
from jax.experimental import pallas as pl
from jax.experimental.pallas import tpu as pltpu
from jax.sharding import PartitionSpec as P

PAD_CONDUCTANCE = 20.0
MESH = pl.DeviceIdType.MESH
VMEM = pltpu.VMEM
LANES = 128
SUB = 8
OUTER, INNER = 0, 1


def word_plan(sizes):
    n_gx, n_gy, _ = sizes
    plan, reach = [], 1
    while reach < n_gx // 2:
        plan.append(("gx", reach))
        reach *= 2
    stride = 1
    while stride - 1 < n_gy // 2:
        plan.append(("gy", stride))
        stride *= 2
    return plan


def kernel(
    sizes, chunks,
    load_hbm, sink_hbm, pad_hbm, plane_hbm, via_hbm, plane_tab, via_tab,
    volt, res,
    load, sink, pad, plane, via,
    rv, rvx, rp, edge, dsum, ux, u_in, m, b, z0, z1, z2, zx, n0, n1, n2,
    rows_out, rows_in, cols_out, cols_in, side, acc, part, red1,
    load_sem, p_send, p_recv, h_send, h_recv, s1, r1, ready,
):
    z, n = (z0, z1, z2), (n0, n1, n2)
    n_gx, n_gy, n_gz = sizes
    _, n_rows, n_cols = plane.shape
    groups = n_rows // SUB
    per = groups // chunks
    early = chunks // 2
    span = per * SUB
    last = n_cols - LANES
    gx, gy, gz = lax.axis_index("gx"), lax.axis_index("gy"), lax.axis_index("gz")
    is_bottom = gz == 0
    is_top = gz == n_gz - 1
    layer = {OUTER: gz, INNER: 1 - gz}
    partner = {"gz": 1 - gz}
    east, west = {"gx": lax.rem(gx + 1, n_gx)}, {"gx": lax.rem(gx + n_gx - 1, n_gx)}
    north, south = {"gy": lax.rem(gy + 1, n_gy)}, {"gy": lax.rem(gy + n_gy - 1, n_gy)}

    loads = [
        pltpu.make_async_copy(src, dst, load_sem.at[i])
        for i, (src, dst) in enumerate(
            (
                (via_hbm.at[layer[INNER]], via.at[layer[INNER]]), (plane_hbm, plane),
                (via_hbm.at[layer[OUTER]], via.at[layer[OUTER]]),
                (pad_hbm, pad), (load_hbm, load), (sink_hbm, sink),
            )
        )
    ]
    for copy in loads:
        copy.start()

    total_count = n_gx * n_gy * n_gz
    mine = (gx * n_gy + gy) * n_gz + gz
    everyone = []
    for d in range(1, total_count):
        other = lax.rem(mine + d, total_count)
        everyone.append({
            "gx": other // (n_gy * n_gz), "gy": lax.rem(other // n_gz, n_gy),
            "gz": lax.rem(other, n_gz),
        })

    def around(axis, at, size, stride):
        ahead = {axis: lax.rem(at + stride, size)}
        behind = {axis: lax.rem(at + size - stride, size)}
        return [ahead] if 2 * stride == size else [ahead, behind]

    nearby = [partner] + around("gy", gy, n_gy, 1) + around("gx", gx, n_gx, 1)
    barrier = pltpu.get_barrier_semaphore()
    for peer in nearby:
        pl.semaphore_signal(barrier, inc=1, device_id=peer, device_id_type=MESH)

    stages = [around(axis, at, size, stride) for axis, at, size, stride in (
        ("gx", gx, n_gx, s) if a == "gx" else ("gy", gy, n_gy, s) for a, s in word_plan(sizes)
    )] + [[partner]]
    told = [0]

    def spread():
        if 0 < told[0] <= len(stages):
            pl.semaphore_wait(ready.at[told[0] - 1], len(stages[told[0] - 1]))
        if told[0] < len(stages):
            for peer in stages[told[0]]:
                pl.semaphore_signal(
                    ready.at[told[0]], inc=1, device_id=peer, device_id_type=MESH
                )
        told[0] += 1

    lane = lax.broadcasted_iota(jnp.int32, (SUB, LANES), 1)
    wide = lax.broadcasted_iota(jnp.int32, (SUB, n_cols), 0)
    acc[...] = jnp.zeros_like(acc)
    cols_out[...] = jnp.zeros_like(cols_out)
    rows_out[...] = jnp.zeros_like(rows_out)

    def tile(j):
        return pl.ds(pl.multiple_of(j * SUB, SUB), SUB)

    def inside(j):
        return pl.ds(pl.multiple_of(j * SUB + SUB, SUB), SUB)

    def each(first, count, body, unroll=1):
        def step(i, carry):
            for u in range(wide_step):
                body(first + i * wide_step + u)
            return carry

        wide_step = unroll if count % unroll == 0 else 1
        lax.fori_loop(0, count // wide_step, step, 0)

    def halves(table, which):
        row = 0.5 / table[pl.ds(layer[which], 1), :]
        return [jnp.broadcast_to(row[:, k:k + 1], (SUB, LANES)) for k in range(table.shape[1])]

    def pick(classes, values):
        out = []
        for s in range(0, n_cols, LANES):
            c = classes[:, s:s + LANES]
            level = list(values)
            bit = 1
            while len(level) > 1:
                on = (c & bit) != 0
                level = [jnp.where(on, level[i + 1], level[i]) for i in range(0, len(level), 2)]
                bit *= 2
            out.append(level[0])
        return jnp.concatenate(out, axis=1)

    def fold(x):
        total = x[:, :LANES]
        for s in range(LANES, n_cols, LANES):
            total = total + x[:, s:s + LANES]
        return total

    def plane_copy(e, c, src, dst):
        return pltpu.make_async_remote_copy(
            src_ref=src, dst_ref=dst, send_sem=p_send.at[e, c], recv_sem=p_recv.at[e, c],
            device_id=partner, device_id_type=MESH,
        )

    def chunk(c):
        return pl.ds(c * span, span)

    def via_copy(c):
        return plane_copy(0, c, rv.at[chunk(c)], rvx.at[chunk(c)])

    def field_copy(k, c):
        return plane_copy(
            k + 1, c, z[k].at[INNER, pl.ds(SUB + c * span, span)], zx.at[k, chunk(c)]
        )

    def save_cols(e, which, j, tiles):
        rows = pl.ds(which * SUB, SUB)
        here = lane == j
        right = pltpu.roll(tiles[:, last:], j + 1, 1)
        left = pltpu.roll(tiles[:, :LANES], j, 1)
        cols_out[e, 0, rows] = jnp.where(here, right, cols_out[e, 0, rows])
        cols_out[e, 1, rows] = jnp.where(here, left, cols_out[e, 1, rows])

    def halo_copies(e):
        made = []
        plan = (
            (rows_out.at[e, 0], rows_in.at[e, 0], north),
            (rows_out.at[e, 1], rows_in.at[e, 1], south),
            (cols_out.at[e, 0], cols_in.at[e, 0], east),
            (cols_out.at[e, 1], cols_in.at[e, 1], west),
        )
        for i, (src, dst, peer) in enumerate(plan):
            made.append(
                pltpu.make_async_remote_copy(
                    src_ref=src, dst_ref=dst, send_sem=h_send.at[e, i],
                    recv_sem=h_recv.at[e, i], device_id=peer, device_id_type=MESH,
                )
            )
        return made

    def save_rows(e, field):
        for which in (OUTER, INNER):
            rows_out[e, 0, which:which + 1] = field[which, SUB + n_rows - 1:SUB + n_rows]
            rows_out[e, 1, which:which + 1] = field[which, SUB:SUB + 1]

    def send_halo(e, field):
        save_rows(e, field)
        for copy in halo_copies(e):
            copy.start()

    def take_halo(e, field):
        for copy in halo_copies(e):
            copy.wait_recv()
        for which in (OUTER, INNER):
            field[which, SUB - 1:SUB] = rows_in[e, 0, which:which + 1]
            field[which, SUB + n_rows:SUB + n_rows + 1] = rows_in[e, 1, which:which + 1]

    def neighbours(e, field, which, j, sides=True):
        here = field[which, inside(j)]
        below = field[which, tile(j)]
        above = field[which, tile(j + 2)]
        to_south = jnp.where(wide == 0, pltpu.roll(below, 1, 0), pltpu.roll(here, 1, 0))
        to_north = jnp.where(
            wide == SUB - 1, pltpu.roll(above, SUB - 1, 0), pltpu.roll(here, SUB - 1, 0)
        )
        rows = pl.ds(which * SUB, SUB)
        from_west = from_east = 0.0
        if sides:
            from_west = pltpu.roll(cols_in[e, 0, rows], lax.rem(LANES - j, LANES), 1)
            from_east = pltpu.roll(cols_in[e, 1, rows], LANES - 1 - j, 1)
        shifted = pltpu.roll(here, 1, 1)
        to_west = jnp.concatenate(
            [jnp.where(lane == 0, from_west, shifted[:, :LANES]), shifted[:, LANES:]], axis=1
        )
        shifted = pltpu.roll(here, n_cols - 1, 1)
        to_east = jnp.concatenate(
            [shifted[:, :last], jnp.where(lane == LANES - 1, from_east, shifted[:, last:])], axis=1
        )
        return here, to_east, to_west, to_north, to_south

    for which in (OUTER, INNER):
        z2[which, :SUB] = jnp.zeros((SUB, n_cols), jnp.float32)
        z2[which, SUB + n_rows:] = jnp.zeros((SUB, n_cols), jnp.float32)

    loads[0].wait()
    table = halves(via_tab, INNER)

    def look_via(j):
        rv[tile(j)] = pick(via[layer[INNER], tile(j)], table)

    each(0, groups, look_via, 3)
    loads[1].wait()
    for which in (OUTER, INNER):
        plane_table = halves(plane_tab, which)

        def look_plane(j, which=which, plane_table=plane_table):
            found = pick(plane[layer[which], tile(j)], plane_table)
            rp[which, inside(j)] = found
            save_cols(0, which, j, found)

        each(0, groups, look_plane, 3)
    save_rows(0, rp)
    loads[2].wait()
    outer_table = halves(via_tab, OUTER)

    def look_outer(j):
        u_in[tile(j)] = 1.0 / (rv[tile(j)] + pick(via[layer[OUTER], tile(j)], outer_table))

    each(0, groups, look_outer, 3)
    for copy in loads[3:]:
        copy.wait()

    pl.semaphore_wait(barrier, len(nearby))
    for c in range(chunks):
        via_copy(c).start()
    for copy in halo_copies(0):
        copy.start()
    spread()
    top_pad = jnp.where(is_top, jnp.float32(PAD_CONDUCTANCE), jnp.float32(0.0))
    bottom_on = jnp.where(is_bottom, jnp.float32(1.0), jnp.float32(0.0))
    take_halo(0, rp)
    spread()
    near = lax.broadcasted_iota(jnp.int32, (2 * SUB, LANES), 1) < groups
    for i in range(2):
        both = jnp.where(near, cols_out[0, 1 - i] + cols_in[0, i], 1.0)
        side[i] = jnp.where(near, 1.0 / both, 0.0)

    def make_edges(j):
        for which in (OUTER, INNER):
            here, e, w, nn, s = neighbours(0, rp, which, j)
            total = None
            for i, other in enumerate((e, w, nn, s)):
                value = 1.0 / (here + other)
                edge[which, i, tile(j)] = value
                total = value if total is None else total + value
            total = total + u_in[tile(j)]
            if which == OUTER:
                total = total + top_pad * pad[tile(j)].astype(jnp.float32)
            dsum[which, tile(j)] = total
        b[tile(j)] = bottom_on * (sink[tile(j)].astype(jnp.float32) * load[tile(j)])

    each(0, groups, make_edges)

    @pl.when(is_bottom)
    def _():
        zx[0] = jnp.zeros_like(zx[0])

    def start_field(j):
        across = 1.0 / (rv[tile(j)] + rvx[tile(j)])
        ux[tile(j)] = across
        d_outer = dsum[OUTER, tile(j)]
        d_inner = dsum[INNER, tile(j)] + across
        joint = u_in[tile(j)]
        inverse = 1.0 / (d_outer * d_inner - joint * joint)
        oo, oi, ii = d_inner * inverse, joint * inverse, d_outer * inverse
        m[0, tile(j)] = oo
        m[1, tile(j)] = oi
        m[2, tile(j)] = ii
        source = b[tile(j)]
        for which, factor in ((OUTER, oo), (INNER, oi)):
            value = factor * source
            z0[which, inside(j)] = value
            save_cols(1, which, j, value)

    for c in range(chunks):
        via_copy(c).wait_recv()
        each(c * per, per, start_field)

        @pl.when(is_bottom)
        def _(c=c):
            field_copy(0, c).start()

    send_halo(1, z0)
    spread()

    def apply(k, j):
        out = []
        for which in (OUTER, INNER):
            here, e, w, nn, s = neighbours(k + 1, z[k], which, j, sides=k < 2)
            value = (
                edge[which, 0, tile(j)] * e + edge[which, 1, tile(j)] * w
                + edge[which, 2, tile(j)] * nn + edge[which, 3, tile(j)] * s
            )
            if which == INNER and k < 2:
                value = value + ux[tile(j)] * zx[k, tile(j)]
            n[k][which, tile(j)] = value
            out.append((here, value))
        return out

    def advance(k, j):
        (z_outer, n_outer), (z_inner, n_inner) = apply(k, j)
        oo, oi, ii = m[0, tile(j)], m[1, tile(j)], m[2, tile(j)]
        next_outer = oo * n_outer + oi * n_inner
        next_inner = oi * n_outer + ii * n_inner
        for which, value in ((OUTER, next_outer), (INNER, next_inner)):
            z[k + 1][which, inside(j)] = value
            save_cols(k + 2, which, j, value)
        if k == 0:
            acc[0] += fold(z_outer * b[tile(j)])
            acc[1] += fold(z_outer * n_outer + z_inner * n_inner)
            acc[2] += fold(next_outer * n_outer + next_inner * n_inner)
        else:
            acc[3] += fold(z_outer * n_outer + z_inner * n_inner)
            acc[4] += fold(next_outer * n_outer + next_inner * n_inner)

    for k in range(2):
        take_halo(k + 1, z[k])
        spread()
        for c in range(chunks):
            if k == 0:
                @pl.when(is_top)
                def _(c=c):
                    field_copy(0, c).wait_recv()
            else:
                field_copy(k, c).wait_recv()
            each(c * per, per, functools.partial(advance, k))
            if k == 0 or c < early:
                field_copy(k + 1, c).start()
            else:
                @pl.when(is_top)
                def _(c=c):
                    field_copy(2, c).start()
        send_halo(k + 2, z[k + 1])

    def finish(j):
        (z_outer, n_outer), (z_inner, n_inner) = apply(2, j)
        acc[5] += fold(z_outer * n_outer + z_inner * n_inner)

    each(0, groups, finish)
    while told[0] <= len(stages):
        spread()

    @pl.when(is_bottom)
    def _():
        def between(j):
            acc[5] += fold(2.0 * z2[INNER, inside(j)] * ux[tile(j)] * zx[2, tile(j)])

        for c in range(chunks):
            field_copy(2, c).wait_recv()
            each(c * per, per, between, 3)

    for copy in halo_copies(3):
        copy.wait_recv()
    end = n_rows - 1
    for i in range(2):
        side[i] = side[i] * cols_in[3, i]
    across_cols = cols_out[3, 1] * side[0] + cols_out[3, 0] * side[1]
    acc[5] += across_cols[:SUB] + across_cols[SUB:]
    for which in (OUTER, INNER):
        from_south = edge[which, 3, 0:1] * rows_in[3, 0, which:which + 1]
        from_north = edge[which, 2, end:n_rows] * rows_in[3, 1, which:which + 1]
        n2[which, 0:1] += from_south
        n2[which, end:n_rows] += from_north
        acc[5, 0:1] += fold(
            z2[which, SUB:SUB + 1] * from_south + z2[which, SUB + end:SUB + n_rows] * from_north
        )

    mix = jnp.zeros((SUB, LANES), jnp.float32)
    for k in range(6):
        total = jnp.sum(jnp.sum(acc[k], axis=0, keepdims=True), axis=1, keepdims=True)
        mix = jnp.where(lane == k, jnp.broadcast_to(total, (SUB, LANES)), mix)
    part[...] = mix[:1]
    red1[mine] = mix[:1]
    first = []
    for d, peer in enumerate(everyone):
        copy = pltpu.make_async_remote_copy(
            src_ref=part, dst_ref=red1.at[mine], send_sem=s1.at[d], recv_sem=r1.at[d],
            device_id=peer, device_id_type=MESH,
        )
        copy.start()
        first.append(copy)

    @pl.when(is_bottom)
    def _():
        for c in range(early, chunks):
            field_copy(2, c).start()

    def mend(j):
        for which in (OUTER, INNER):
            rows = pl.ds(which * SUB, SUB)
            from_west = pltpu.roll(side[0, rows], lax.rem(LANES - j, LANES), 1)
            from_east = pltpu.roll(side[1, rows], LANES - 1 - j, 1)
            n2[which, tile(j), :LANES] += jnp.where(lane == 0, from_west, 0.0)
            n2[which, tile(j), last:] += jnp.where(lane == LANES - 1, from_east, 0.0)

    each(0, groups, mend)
    for copy in first:
        copy.wait_recv()
    mix = red1[0]
    for i in range(1, total_count):
        mix = mix + red1[i]
    nu = [jnp.broadcast_to(mix[0:1, k:k + 1], (SUB, LANES)) for k in range(6)]
    h = [nu[k] - nu[k + 1] for k in range(5)]
    l10 = h[1] / h[0]
    d1 = h[2] - l10 * h[1]
    l20 = h[2] / h[0]
    t = h[3] - l10 * h[2]
    l21 = t / d1
    d2 = h[4] - l20 * h[2] - l21 * t
    y0 = nu[0]
    y1 = nu[1] - l10 * y0
    y2 = nu[2] - l20 * y0 - l21 * y1
    c2 = y2 / d2
    c1 = y1 / d1 - l21 * c2
    c0 = y0 / h[0] - l10 * c1 - l20 * c2

    def full(x):
        return jnp.concatenate([x] * (n_cols // LANES), axis=1)

    w0, w1, w2 = full(c0), full(c1), full(c2)
    rb, r0, rr1 = 1.0 - w0, w0 - w1, w1 - w2

    def emit(j):
        for which in (OUTER, INNER):
            volt[layer[which], tile(j)] = (
                w0 * z0[which, inside(j)] + w1 * z1[which, inside(j)]
                + w2 * z2[which, inside(j)]
            )
            tail = n2[which, tile(j)]
            if which == INNER:
                tail = tail + ux[tile(j)] * zx[2, tile(j)]
            value = r0 * n0[which, tile(j)] + rr1 * n1[which, tile(j)] + w2 * tail
            if which == OUTER:
                value = value + rb * b[tile(j)]
            res[layer[which], tile(j)] = value

    for c in range(chunks):
        @pl.when(is_top)
        def _(c=c):
            field_copy(2, c).wait_recv()
        each(c * per, per, emit, 3)

    for c in range(chunks):
        via_copy(c).wait_send()

        @pl.when(is_bottom)
        def _(c=c):
            field_copy(0, c).wait_send()
        field_copy(1, c).wait_send()
        field_copy(2, c).wait_send()
    for e in range(4):
        for copy in halo_copies(e):
            copy.wait_send()
    for copy in first:
        copy.wait_send()


def store(volt, res, volt_hbm, res_hbm, sem):
    copies = [
        pltpu.make_async_copy(src.at[k], dst.at[k], sem.at[i, k])
        for i, (src, dst) in enumerate(((volt, volt_hbm), (res, res_hbm)))
        for k in range(src.shape[0])
    ]
    for copy in copies:
        copy.start()
    for copy in copies:
        copy.wait()


def solution(mesh):
    sizes = tuple(mesh.shape[a] for a in ("gx", "gy", "gz"))
    n_gx, n_gy, n_gz = sizes

    def shards(load_current, sink_mask, pad_mask, plane_class, via_class, plane_table, via_table):
        n_layers, rows, cols = plane_class.shape
        groups = rows // SUB
        assert n_layers == 2 and n_gz == 2 and groups <= LANES
        chunks = max(c for c in range(1, 9) if groups % c == 0)
        f32, i32 = jnp.float32, jnp.int32
        dma = pltpu.SemaphoreType.DMA
        hbm = pl.BlockSpec(memory_space=pl.ANY)
        vmem = pl.BlockSpec(memory_space=VMEM)
        shape = (n_layers, rows, cols)
        padded = (2, rows + 2 * SUB, cols)
        flat = VMEM((rows, cols), f32)
        volt, res = pl.pallas_call(
            functools.partial(kernel, sizes, chunks),
            out_shape=(VMEM(shape, f32), VMEM(shape, f32)),
            in_specs=[hbm] * 5 + [vmem] * 2,
            out_specs=(vmem, vmem),
            scratch_shapes=[
                flat, VMEM((rows, cols), i32), VMEM((rows, cols), i32),
                VMEM((2, rows, cols), i32), VMEM((2, rows, cols), i32),
                flat, flat, VMEM(padded, f32), VMEM((2, 4, rows, cols), f32),
                VMEM((2, rows, cols), f32), flat, flat, VMEM((3, rows, cols), f32), flat,
                VMEM(padded, f32), VMEM(padded, f32), VMEM(padded, f32),
                VMEM((3, rows, cols), f32), VMEM((2, rows, cols), f32),
                VMEM((2, rows, cols), f32), VMEM((2, rows, cols), f32),
                VMEM((4, 2, SUB, cols), f32), VMEM((4, 2, SUB, cols), f32),
                VMEM((4, 2, 2 * SUB, LANES), f32), VMEM((4, 2, 2 * SUB, LANES), f32),
                VMEM((2, 2 * SUB, LANES), f32),
                VMEM((6, SUB, LANES), f32), VMEM((1, LANES), f32),
                VMEM((n_gx * n_gy * n_gz, 1, LANES), f32),
                dma((6,)), dma((4, chunks)), dma((4, chunks)),
                dma((4, 4)), dma((4, 4)),
                dma((n_gx * n_gy * n_gz - 1,)), dma((n_gx * n_gy * n_gz - 1,)),
                pltpu.SemaphoreType.REGULAR((len(word_plan(sizes)) + 1,)),
            ],
            compiler_params=pltpu.CompilerParams(
                collective_id=0, has_side_effects=True, vmem_limit_bytes=60 * 1024 * 1024
            ),
            name="grid_cg",
        )(load_current, sink_mask, pad_mask, plane_class, via_class, plane_table, via_table)
        whole = jax.ShapeDtypeStruct(shape, f32)
        return pl.pallas_call(
            store,
            out_shape=(whole, whole),
            in_specs=[vmem] * 2,
            out_specs=(hbm, hbm),
            scratch_shapes=[dma((2, n_layers))],
            name="store",
        )(*(pltpu.with_memory_space_constraint(x, VMEM) for x in (volt, res)))

    in_specs = (
        P("gy", "gx"), P("gy", "gx"), P("gy", "gx"),
        P("gz", "gy", "gx"), P("gz", "gy", "gx"), P("gz", None), P("gz", None),
    )
    out_specs = (P("gz", "gy", "gx"), P("gz", "gy", "gx"))
    return jax.shard_map(shards, mesh=mesh, in_specs=in_specs, out_specs=out_specs, check_vma=False)
```

profile of v0, /device:TPU:0, one launch (start us, length us, event | category | flops | bytes accessed | tf_op | source)
XLA Modules:
  0.0 48.3 jit_solution(10319596476933645314)
XLA Ops:
  0.6 46.5 %grid_cg.1 = (f32[2,192,512]{2,1,0:T(8,128)S(1)}, f32[2,192,512]{2,1,0:T(8,128)S(1)}) custom-call(f32[192,512]{1,0:T(8,128)} %load_hbm.1, s32[192,512]{1,0:T(8,128)} %sink_hbm.1, s32[192,512]{1,0:T(8,128)} %pad_hbm.1, s32[2,192,512]{2,1,0:T(8,128)} %plane_hbm.1, s32[2,192,512]{2,1,0:T(8,128)} %via_hbm.1, f32[2,8]{1,0:T(2,128)} %plane_tab.1, f32[2,8]{1,0:T(2,128)} %via_tab.1), custom_call_target="tpu_custom_call" | custom-call | tf_op jit(solution)/shard_map/grid_cg/pallas_call | solution.py:525
  47.2 1.2 %store.1 = (f32[2,192,512]{2,1,0:T(8,128)}, f32[2,192,512]{2,1,0:T(8,128)}) custom-call(f32[2,192,512]{2,1,0:T(8,128)S(1)} %get-tuple-element.4.volt, f32[2,192,512]{2,1,0:T(8,128)S(1)} %get-tuple-element.5.res), custom_call_target="tpu_custom_call" | custom-call | tf_op jit(solution)/shard_map/store/pallas_call | solution.py:554
where the time goes:
time: 48.5 us; the launch traced here: 48.3 us
  Pallas kernels  47.7 us (98%)
  between operations  0.64 us (1%)
    pallas_call x1, Pallas kernels, shards(): pl.pallas_call(functools.partial(kernel, sizes, chunks), out_shape=(VMEM(...  46.5 us
    pallas_call x1, Pallas kernels, shards(): pl.pallas_call(store, out_shape=(whole, whole), in_specs=[vmem] * 2, out_...  1.17 us

commit v1 on v0

--- a/solution.py
+++ b/solution.py
@@ -34,15 +34,16 @@
     volt, res,
     load, sink, pad, plane, via,
     rv, rvx, rp, edge, dsum, ux, u_in, m, b, z0, z1, z2, zx, n0, n1, n2,
-    rows_out, rows_in, cols_out, cols_in, side, acc, part, red1,
-    load_sem, p_send, p_recv, h_send, h_recv, s1, r1, ready,
+    rows_out, rows_in, cols_out, cols_in, side, passed, acc, part, red,
+    load_sem, p_send, p_recv, h_send, h_recv, f_send, f_recv, s1, r1, ready,
 ):
     z, n = (z0, z1, z2), (n0, n1, n2)
     n_gx, n_gy, n_gz = sizes
     _, n_rows, n_cols = plane.shape
     groups = n_rows // SUB
     per = groups // chunks
-    early = chunks // 2
+    middle = chunks - 2
+    early = chunks * 3 // 4 - 2
     span = per * SUB
     last = n_cols - LANES
     gx, gy, gz = lax.axis_index("gx"), lax.axis_index("gy"), lax.axis_index("gz")
@@ -121,6 +122,16 @@
 
         wide_step = unroll if count % unroll == 0 else 1
         lax.fori_loop(0, count // wide_step, step, 0)
+
+    def loop(count, body, first=0):
+        def step(i, carry):
+            body(i)
+            return carry
+
+        lax.fori_loop(first, count, step, 0)
+
+    def end(i):
+        return i * (chunks - 1)
 
     def halves(table, which):
         row = 0.5 / table[pl.ds(layer[which], 1), :]
@@ -151,15 +162,15 @@
             device_id=partner, device_id_type=MESH,
         )
 
-    def chunk(c):
-        return pl.ds(c * span, span)
+    def chunk(c, pad=0):
+        return pl.ds(pl.multiple_of(pad + c * span, SUB), span)
 
     def via_copy(c):
         return plane_copy(0, c, rv.at[chunk(c)], rvx.at[chunk(c)])
 
     def field_copy(k, c):
         return plane_copy(
-            k + 1, c, z[k].at[INNER, pl.ds(SUB + c * span, span)], zx.at[k, chunk(c)]
+            k + 1, c, z[k].at[INNER, chunk(c, SUB)], zx.at[k, chunk(c)]
         )
 
     def save_cols(e, which, j, tiles):
@@ -197,12 +208,30 @@
         for copy in halo_copies(e):
             copy.start()
 
-    def take_halo(e, field):
-        for copy in halo_copies(e):
+    def take_rows(e, field):
+        for copy in halo_copies(e)[:2]:
             copy.wait_recv()
         for which in (OUTER, INNER):
             field[which, SUB - 1:SUB] = rows_in[e, 0, which:which + 1]
             field[which, SUB + n_rows:SUB + n_rows + 1] = rows_in[e, 1, which:which + 1]
+
+    def take_cols(e):
+        for copy in halo_copies(e)[2:]:
+            copy.wait_recv()
+
+    def take_halo(e, field):
+        take_rows(e, field)
+        take_cols(e)
+
+    def pass_copies():
+        return [
+            pltpu.make_async_remote_copy(
+                src_ref=cols_in.at[1, i, pl.ds(SUB, SUB)], dst_ref=passed.at[i],
+                send_sem=f_send.at[i], recv_sem=f_recv.at[i],
+                device_id=partner, device_id_type=MESH,
+            )
+            for i in range(2)
+        ]
 
     def neighbours(e, field, which, j, sides=True):
         here = field[which, inside(j)]
@@ -260,12 +289,12 @@
         copy.wait()
 
     pl.semaphore_wait(barrier, len(nearby))
-    for c in range(chunks):
-        via_copy(c).start()
     for copy in halo_copies(0):
         copy.start()
+    loop(chunks, lambda c: via_copy(c).start())
     spread()
     top_pad = jnp.where(is_top, jnp.float32(PAD_CONDUCTANCE), jnp.float32(0.0))
+    top_on = jnp.where(is_top, jnp.float32(1.0), jnp.float32(0.0))
     bottom_on = jnp.where(is_bottom, jnp.float32(1.0), jnp.float32(0.0))
     take_halo(0, rp)
     spread()
@@ -288,11 +317,8 @@
             dsum[which, tile(j)] = total
         b[tile(j)] = bottom_on * (sink[tile(j)].astype(jnp.float32) * load[tile(j)])
 
-    each(0, groups, make_edges)
-
-    @pl.when(is_bottom)
-    def _():
-        zx[0] = jnp.zeros_like(zx[0])
+    each(0, groups, make_edges, 3)
+    spread()
 
     def start_field(j):
         across = 1.0 / (rv[tile(j)] + rvx[tile(j)])
@@ -309,17 +335,28 @@
         for which, factor in ((OUTER, oo), (INNER, oi)):
             value = factor * source
             z0[which, inside(j)] = value
-            save_cols(1, which, j, value)
-
-    for c in range(chunks):
+            response = (m[1 + which, tile(j)] * across) * top_on
+            save_cols(1, which, j, value + response)
+
+    def open_chunk(c):
         via_copy(c).wait_recv()
-        each(c * per, per, start_field)
+        each(c * per, per, start_field, 3)
 
         @pl.when(is_bottom)
-        def _(c=c):
+        def _():
             field_copy(0, c).start()
 
-    send_halo(1, z0)
+    loop(chunks, open_chunk)
+
+    @pl.when(is_bottom)
+    def _():
+        send_halo(1, z0)
+
+    @pl.when(is_top)
+    def _():
+        for copy in halo_copies(1)[2:]:
+            copy.start()
+
     spread()
 
     def apply(k, j):
@@ -330,7 +367,7 @@
                 edge[which, 0, tile(j)] * e + edge[which, 1, tile(j)] * w
                 + edge[which, 2, tile(j)] * nn + edge[which, 3, tile(j)] * s
             )
-            if which == INNER and k < 2:
+            if which == INNER and k == 1:
                 value = value + ux[tile(j)] * zx[k, tile(j)]
             n[k][which, tile(j)] = value
             out.append((here, value))
@@ -352,77 +389,130 @@
             acc[3] += fold(z_outer * n_outer + z_inner * n_inner)
             acc[4] += fold(next_outer * n_outer + next_inner * n_inner)
 
-    for k in range(2):
-        take_halo(k + 1, z[k])
+    def begin(j):
+        joint = ux[tile(j)] * zx[0, tile(j)]
+        n0[OUTER, tile(j)] = jnp.zeros_like(joint)
+        n0[INNER, tile(j)] = joint
+        inner = m[2, tile(j)] * joint
+        z1[OUTER, inside(j)] = m[1, tile(j)] * joint
+        z1[INNER, inside(j)] = inner
+        acc[2] += fold(inner * joint)
+
+    @pl.when(is_top)
+    def _():
+        def begin_chunk(c):
+            field_copy(0, c).wait_recv()
+            each(c * per, per, begin, 3)
+            field_copy(1, c).start()
+
+        loop(chunks, begin_chunk)
+        save_rows(2, z1)
+        for copy in halo_copies(2)[:2]:
+            copy.start()
+        take_cols(1)
+        for i, copy in enumerate(pass_copies()):
+            copy.wait_recv()
+            cols_in[2, i] = cols_in[1, i] * jnp.concatenate([passed[i], passed[i]], axis=0)
+
+    @pl.when(is_bottom)
+    def _():
+        take_halo(1, z0)
+        for copy in pass_copies():
+            copy.start()
+        def first_chunk(c):
+            each(c * per, per, functools.partial(advance, 0), 3)
+            field_copy(1, c).start()
+
+        loop(chunks, lambda i: first_chunk(lax.rem(i + 1, chunks)))
+        send_halo(2, z1)
+        take_cols(2)
+
+    while told[0] <= len(stages):
         spread()
-        for c in range(chunks):
-            if k == 0:
-                @pl.when(is_top)
-                def _(c=c):
-                    field_copy(0, c).wait_recv()
-            else:
-                field_copy(k, c).wait_recv()
-            each(c * per, per, functools.partial(advance, k))
-            if k == 0 or c < early:
-                field_copy(k + 1, c).start()
-            else:
-                @pl.when(is_top)
-                def _(c=c):
-                    field_copy(2, c).start()
-        send_halo(k + 2, z[k + 1])
+
+    def second_chunk(c):
+        field_copy(1, c).wait_recv()
+        each(c * per, per, functools.partial(advance, 1), 3)
+
+        @pl.when(is_top)
+        def _():
+            field_copy(2, c).start()
+
+    loop(middle, lambda i: second_chunk(i + 1))
+    take_rows(2, z1)
+    loop(2, lambda i: second_chunk(end(1 - i)))
+
+    @pl.when(is_bottom)
+    def _():
+        loop(2, lambda i: field_copy(2, end(i)).start())
+        loop(early, lambda i: field_copy(2, middle - i).start())
+
+    send_halo(3, z2)
+
+    def put(mix, k):
+        total = jnp.sum(jnp.sum(acc[k], axis=0, keepdims=True), axis=1, keepdims=True)
+        return jnp.where(lane == k, jnp.broadcast_to(total, (SUB, LANES)), mix)
+
+    def sum_copies():
+        return [
+            pltpu.make_async_remote_copy(
+                src_ref=part, dst_ref=red.at[mine], send_sem=s1.at[d], recv_sem=r1.at[d],
+                device_id=peer, device_id_type=MESH,
+            )
+            for d, peer in enumerate(everyone)
+        ]
 
     def finish(j):
         (z_outer, n_outer), (z_inner, n_inner) = apply(2, j)
         acc[5] += fold(z_outer * n_outer + z_inner * n_inner)
 
-    each(0, groups, finish)
-    while told[0] <= len(stages):
-        spread()
+    each(0, groups, finish, 3)
+
+    mix = jnp.zeros((SUB, LANES), jnp.float32)
+    for k in range(5):
+        mix = put(mix, k)
+
+    def between(j):
+        acc[5] += fold(2.0 * z2[INNER, inside(j)] * ux[tile(j)] * zx[2, tile(j)])
+
+    def between_chunk(c):
+        field_copy(2, c).wait_recv()
+        each(c * per, per, between, 3)
+
+    @pl.when(is_top)
+    def _():
+        loop(2, lambda i: between_chunk(end(i)))
 
     @pl.when(is_bottom)
     def _():
-        def between(j):
-            acc[5] += fold(2.0 * z2[INNER, inside(j)] * ux[tile(j)] * zx[2, tile(j)])
-
-        for c in range(chunks):
-            field_copy(2, c).wait_recv()
-            each(c * per, per, between, 3)
+        loop(middle, lambda i: between_chunk(i + 1))
 
     for copy in halo_copies(3):
         copy.wait_recv()
-    end = n_rows - 1
+    edge_row = n_rows - 1
     for i in range(2):
         side[i] = side[i] * cols_in[3, i]
     across_cols = cols_out[3, 1] * side[0] + cols_out[3, 0] * side[1]
     acc[5] += across_cols[:SUB] + across_cols[SUB:]
     for which in (OUTER, INNER):
         from_south = edge[which, 3, 0:1] * rows_in[3, 0, which:which + 1]
-        from_north = edge[which, 2, end:n_rows] * rows_in[3, 1, which:which + 1]
+        from_north = edge[which, 2, edge_row:n_rows] * rows_in[3, 1, which:which + 1]
         n2[which, 0:1] += from_south
-        n2[which, end:n_rows] += from_north
+        n2[which, edge_row:n_rows] += from_north
         acc[5, 0:1] += fold(
-            z2[which, SUB:SUB + 1] * from_south + z2[which, SUB + end:SUB + n_rows] * from_north
-        )
-
-    mix = jnp.zeros((SUB, LANES), jnp.float32)
-    for k in range(6):
-        total = jnp.sum(jnp.sum(acc[k], axis=0, keepdims=True), axis=1, keepdims=True)
-        mix = jnp.where(lane == k, jnp.broadcast_to(total, (SUB, LANES)), mix)
+            z2[which, SUB:SUB + 1] * from_south + z2[which, SUB + edge_row:SUB + n_rows] * from_north
+        )
+
+    mix = put(mix, 5)
     part[...] = mix[:1]
-    red1[mine] = mix[:1]
-    first = []
-    for d, peer in enumerate(everyone):
-        copy = pltpu.make_async_remote_copy(
-            src_ref=part, dst_ref=red1.at[mine], send_sem=s1.at[d], recv_sem=r1.at[d],
-            device_id=peer, device_id_type=MESH,
-        )
+    red[mine] = mix[:1]
+    sums = sum_copies()
+    for copy in sums:
         copy.start()
-        first.append(copy)
 
     @pl.when(is_bottom)
     def _():
-        for c in range(early, chunks):
-            field_copy(2, c).start()
+        loop(middle, lambda i: field_copy(2, middle - i).start(), early)
 
     def mend(j):
         for which in (OUTER, INNER):
@@ -432,12 +522,13 @@
             n2[which, tile(j), :LANES] += jnp.where(lane == 0, from_west, 0.0)
             n2[which, tile(j), last:] += jnp.where(lane == LANES - 1, from_east, 0.0)
 
-    each(0, groups, mend)
-    for copy in first:
+    each(0, groups, mend, 6)
+    for copy in sums:
         copy.wait_recv()
-    mix = red1[0]
-    for i in range(1, total_count):
-        mix = mix + red1[i]
+    rows = [red[i] for i in range(total_count)]
+    while len(rows) > 1:
+        rows = [sum(rows[i:i + 2][1:], rows[i]) for i in range(0, len(rows), 2)]
+    mix = rows[0]
     nu = [jnp.broadcast_to(mix[0:1, k:k + 1], (SUB, LANES)) for k in range(6)]
     h = [nu[k] - nu[k + 1] for k in range(5)]
     l10 = h[1] / h[0]
@@ -445,11 +536,10 @@
     l20 = h[2] / h[0]
     t = h[3] - l10 * h[2]
     l21 = t / d1
-    d2 = h[4] - l20 * h[2] - l21 * t
     y0 = nu[0]
     y1 = nu[1] - l10 * y0
     y2 = nu[2] - l20 * y0 - l21 * y1
-    c2 = y2 / d2
+    c2 = y2 / (h[4] - l20 * h[2] - l21 * t)
     c1 = y1 / d1 - l21 * c2
     c0 = y0 / h[0] - l10 * c1 - l20 * c2
 
@@ -473,24 +563,35 @@
                 value = value + rb * b[tile(j)]
             res[layer[which], tile(j)] = value
 
-    for c in range(chunks):
-        @pl.when(is_top)
-        def _(c=c):
+    def emit_chunk(c, other):
+        @pl.when(other)
+        def _():
             field_copy(2, c).wait_recv()
+
         each(c * per, per, emit, 3)
 
-    for c in range(chunks):
+    loop(2, lambda i: emit_chunk(end(i), is_bottom))
+    loop(middle, lambda i: emit_chunk(middle - i, is_top))
+
+    def drain(c):
         via_copy(c).wait_send()
-
-        @pl.when(is_bottom)
-        def _(c=c):
-            field_copy(0, c).wait_send()
         field_copy(1, c).wait_send()
         field_copy(2, c).wait_send()
-    for e in range(4):
-        for copy in halo_copies(e):
+
+        @pl.when(is_bottom)
+        def _():
+            field_copy(0, c).wait_send()
+
+    loop(chunks, drain)
+    for copy in halo_copies(0) + halo_copies(1)[2:] + halo_copies(2)[:2] + halo_copies(3):
+        copy.wait_send()
+
+    @pl.when(is_bottom)
+    def _():
+        for copy in halo_copies(1)[:2] + halo_copies(2)[2:] + pass_copies():
             copy.wait_send()
-    for copy in first:
+
+    for copy in sums:
         copy.wait_send()
 
 
@@ -514,7 +615,7 @@
         n_layers, rows, cols = plane_class.shape
         groups = rows // SUB
         assert n_layers == 2 and n_gz == 2 and groups <= LANES
-        chunks = max(c for c in range(1, 9) if groups % c == 0)
+        chunks = max(c for c in range(3, 9) if groups % c == 0)
         f32, i32 = jnp.float32, jnp.int32
         dma = pltpu.SemaphoreType.DMA
         hbm = pl.BlockSpec(memory_space=pl.ANY)
@@ -537,11 +638,11 @@
                 VMEM((2, rows, cols), f32), VMEM((2, rows, cols), f32),
                 VMEM((4, 2, SUB, cols), f32), VMEM((4, 2, SUB, cols), f32),
                 VMEM((4, 2, 2 * SUB, LANES), f32), VMEM((4, 2, 2 * SUB, LANES), f32),
-                VMEM((2, 2 * SUB, LANES), f32),
+                VMEM((2, 2 * SUB, LANES), f32), VMEM((2, SUB, LANES), f32),
                 VMEM((6, SUB, LANES), f32), VMEM((1, LANES), f32),
                 VMEM((n_gx * n_gy * n_gz, 1, LANES), f32),
                 dma((6,)), dma((4, chunks)), dma((4, chunks)),
-                dma((4, 4)), dma((4, 4)),
+                dma((4, 4)), dma((4, 4)), dma((2,)), dma((2,)),
                 dma((n_gx * n_gy * n_gz - 1,)), dma((n_gx * n_gy * n_gz - 1,)),
                 pltpu.SemaphoreType.REGULAR((len(word_plan(sizes)) + 1,)),
             ],

time: 48.5 us -> 47.2 us (0.973)
  Pallas kernels: 47.7 us -> 46.3 us
    pallas_call x1, Pallas kernels: 46.5 us -> 45.2 us  [shards(): pl.pallas_call(functools.partial(kernel, sizes, chunks), out_shape=(VMEM(...]
where the time goes in v1:
time: 47.2 us; the launch traced here: 47 us
  Pallas kernels  46.3 us (98%)
  between operations  0.64 us (1%)
    pallas_call x1, Pallas kernels, shards(): pl.pallas_call(functools.partial(kernel, sizes, chunks), out_shape=(VMEM(...  45.2 us
    pallas_call x1, Pallas kernels, shards(): pl.pallas_call(store, out_shape=(whole, whole), in_specs=[vmem] * 2, out_...  1.17 us

profile of v1, /device:TPU:0, one launch (start us, length us, event | category | flops | bytes accessed | tf_op | source)
XLA Modules:
  0.0 47.0 jit_solution(10986395044827913655)
XLA Ops:
  0.6 45.2 %grid_cg.1 = (f32[2,192,512]{2,1,0:T(8,128)S(1)}, f32[2,192,512]{2,1,0:T(8,128)S(1)}) custom-call(f32[192,512]{1,0:T(8,128)} %load_hbm.1, s32[192,512]{1,0:T(8,128)} %sink_hbm.1, s32[192,512]{1,0:T(8,128)} %pad_hbm.1, s32[2,192,512]{2,1,0:T(8,128)} %plane_hbm.1, s32[2,192,512]{2,1,0:T(8,128)} %via_hbm.1, f32[2,8]{1,0:T(2,128)} %plane_tab.1, f32[2,8]{1,0:T(2,128)} %via_tab.1), custom_call_target="tpu_custom_call" | custom-call | tf_op jit(solution)/shard_map/grid_cg/pallas_call | solution.py:626
  45.8 1.2 %store.1 = (f32[2,192,512]{2,1,0:T(8,128)}, f32[2,192,512]{2,1,0:T(8,128)}) custom-call(f32[2,192,512]{2,1,0:T(8,128)S(1)} %get-tuple-element.4.volt, f32[2,192,512]{2,1,0:T(8,128)S(1)} %get-tuple-element.5.res), custom_call_target="tpu_custom_call" | custom-call | tf_op jit(solution)/shard_map/store/pallas_call | solution.py:655

commit v2 on v1

--- a/solution.py
+++ b/solution.py
@@ -43,7 +43,7 @@
     groups = n_rows // SUB
     per = groups // chunks
     middle = chunks - 2
-    early = chunks * 3 // 4 - 2
+    early = middle // 3
     span = per * SUB
     last = n_cols - LANES
     gx, gy, gz = lax.axis_index("gx"), lax.axis_index("gy"), lax.axis_index("gz")
@@ -267,6 +267,9 @@
         rv[tile(j)] = pick(via[layer[INNER], tile(j)], table)
 
     each(0, groups, look_via, 3)
+    pl.semaphore_wait(barrier, len(nearby))
+    loop(chunks, lambda c: via_copy(c).start())
+    spread()
     loads[1].wait()
     for which in (OUTER, INNER):
         plane_table = halves(plane_tab, which)
@@ -278,6 +281,8 @@
 
         each(0, groups, look_plane, 3)
     save_rows(0, rp)
+    for copy in halo_copies(0):
+        copy.start()
     loads[2].wait()
     outer_table = halves(via_tab, OUTER)
 
@@ -288,11 +293,6 @@
     for copy in loads[3:]:
         copy.wait()
 
-    pl.semaphore_wait(barrier, len(nearby))
-    for copy in halo_copies(0):
-        copy.start()
-    loop(chunks, lambda c: via_copy(c).start())
-    spread()
     top_pad = jnp.where(is_top, jnp.float32(PAD_CONDUCTANCE), jnp.float32(0.0))
     top_on = jnp.where(is_top, jnp.float32(1.0), jnp.float32(0.0))
     bottom_on = jnp.where(is_bottom, jnp.float32(1.0), jnp.float32(0.0))

time: 47.2 us -> 45.3 us (0.960)
  Pallas kernels: 46.3 us -> 44.4 us
    pallas_call x1, Pallas kernels: 45.2 us -> 43.3 us  [shards(): pl.pallas_call(functools.partial(kernel, sizes, chunks), out_shape=(VMEM(...]
where the time goes in v2:
time: 45.3 us; the launch traced here: 45.1 us
  Pallas kernels  44.4 us (98%)
  between operations  0.64 us (1%)
    pallas_call x1, Pallas kernels, shards(): pl.pallas_call(functools.partial(kernel, sizes, chunks), out_shape=(VMEM(...  43.3 us
    pallas_call x1, Pallas kernels, shards(): pl.pallas_call(store, out_shape=(whole, whole), in_specs=[vmem] * 2, out_...  1.17 us

profile of v2, /device:TPU:0, one launch (start us, length us, event | category | flops | bytes accessed | tf_op | source)
XLA Modules:
  0.0 45.1 jit_solution(11801063489925259858)
XLA Ops:
  0.6 43.3 %grid_cg.1 = (f32[2,192,512]{2,1,0:T(8,128)S(1)}, f32[2,192,512]{2,1,0:T(8,128)S(1)}) custom-call(f32[192,512]{1,0:T(8,128)} %load_hbm.1, s32[192,512]{1,0:T(8,128)} %sink_hbm.1, s32[192,512]{1,0:T(8,128)} %pad_hbm.1, s32[2,192,512]{2,1,0:T(8,128)} %plane_hbm.1, s32[2,192,512]{2,1,0:T(8,128)} %via_hbm.1, f32[2,8]{1,0:T(2,128)} %plane_tab.1, f32[2,8]{1,0:T(2,128)} %via_tab.1), custom_call_target="tpu_custom_call" | custom-call | tf_op jit(solution)/shard_map/grid_cg/pallas_call | solution.py:626
  43.9 1.2 %store.1 = (f32[2,192,512]{2,1,0:T(8,128)}, f32[2,192,512]{2,1,0:T(8,128)}) custom-call(f32[2,192,512]{2,1,0:T(8,128)S(1)} %get-tuple-element.4.volt, f32[2,192,512]{2,1,0:T(8,128)S(1)} %get-tuple-element.5.res), custom_call_target="tpu_custom_call" | custom-call | tf_op jit(solution)/shard_map/store/pallas_call | solution.py:655
